TPU v7x, 128 devices: a whole 4x4x4 slice. The times are simulated.
128 devices in a mesh: gx: 16 (over y, z), gy: 8 (over x, core).
Axes of the slice: x: 4, y: 4, z: 4, core: 2. Of those that a mesh axis runs over, the one named last changes fastest.
Arguments:
- states: bfloat16 [80, 8, 512, 2048], P('gx', None, 'gy'), may hold values from -6 to 6
- obs_pert: bfloat16 [80, 8, 2048], P(None, 'gy', 'gx'), may hold values from -6 to 6
- obs_innov: bfloat16 [8, 2048], P('gy', 'gx'), may hold values from -6 to 6
- obs_cell: int32 [8, 2048], P('gy', 'gx'), may hold values from 0 to 8191
- obs_count: int32 [8, 16], P('gy', 'gx'), may hold values from 16 to 128, as said below
Outputs:
- analysis: bfloat16 [80, 8, 512, 2048], P(None, None, 'gy', 'gx')
Inputs may be any that keep to these rules, and one draw needn't show every extreme that they name: `obs_count`: at most 128; some tile has exactly 128. `obs_cell`: slots at or after their tile's count are unused.
All inputs are finite; a program needn't handle non-finite values.
Results may differ from a plain program's by a relative error of at most 0.0057.
Values may be sent and summed in bfloat16 or wider, within the bound.
A program may use at most 128 MiB of HBM per device.

v0:
```python
import functools

import jax
import jax.numpy as jnp
from jax import lax
from jax.experimental import pallas as pl
from jax.experimental.pallas import tpu as pltpu
from jax.sharding import PartitionSpec as P

MESH = pl.DeviceIdType.MESH
F32 = jnp.float32
BF16 = jnp.bfloat16

TX = 128
TY = 64
NS_ITERS = 4
RB = 8
PK = 96
LANES = 128


def wrap(value, count):
    return lax.rem(value + count, count)


def split(value):
    high = value.astype(BF16)
    low = (value - high.astype(F32)).astype(BF16)
    return high, low


def tall(value):
    rows = value.shape[0]
    return jnp.concatenate([value, jnp.zeros((LANES - rows, value.shape[1]), value.dtype)], axis=0)


def product(left, right):
    lh, ll = left
    rh, rl = (tall(part) for part in right)
    lhs = jnp.concatenate([lh, ll], axis=1)
    rhs = jnp.concatenate(
        [
            jnp.concatenate([rh, rl], axis=1),
            jnp.concatenate([rh, jnp.zeros_like(rl)], axis=1),
        ],
        axis=0,
    )
    both = jnp.dot(lhs, rhs, preferred_element_type=F32)
    return both[:, :LANES] + both[:, LANES:]


def kernel(
    members,
    levels,
    nrows,
    ncols,
    states,
    packed,
    out,
    fields,
    groups,
    right,
    weighted,
    products,
    tmat,
    spread,
    mixed,
    own_sem,
    state_send,
    state_recv,
    obs_send,
    obs_recv,
):
    col = lax.axis_index("gx")
    row = lax.axis_index("gy")
    share = members // ncols
    chunks = TY // RB

    barrier = pltpu.get_barrier_semaphore()

    def greet(coords):
        pl.semaphore_signal(barrier, inc=1, device_id=coords, device_id_type=MESH)

    for d in range(1, ncols):
        greet({"gx": lax.rem(col + d, ncols)})
    for a in (-1, 1):

        @pl.when(jnp.logical_and(row + a >= 0, row + a < nrows))
        def _():
            for b in (-1, 0, 1):
                greet({"gx": wrap(col + b, ncols), "gy": row + a})

    inner = jnp.logical_and(row > 0, row < nrows - 1)
    pl.semaphore_wait(barrier, ncols - 1 + jnp.where(inner, 6, 3))

    def obs_copy(slot, a, coords):
        return pltpu.make_async_remote_copy(
            src_ref=packed,
            dst_ref=groups.at[slot],
            send_sem=obs_send.at[slot],
            recv_sem=obs_recv.at[a + 1],
            device_id=coords,
            device_id_type=MESH,
        )

    def obs_plain(a, b, act):
        slot = (a + 1) * 3 + b + 1
        if a == 0 and b == 0:
            return

        def go():
            act(obs_copy(slot, a, {"gx": wrap(col - b, ncols), "gy": row - a}))

        if a == 0:
            go()
        else:
            pl.when(jnp.logical_and(row - a >= 0, row - a < nrows))(go)

    def obs_fold(b, act, act_local):
        slot = 6 + b + 1
        target = lax.rem(2 * ncols - 1 + b - col, ncols)
        at_fold = row == nrows - 1

        @pl.when(jnp.logical_and(at_fold, target != col))
        def _():
            act(
                pltpu.make_async_remote_copy(
                    src_ref=packed,
                    dst_ref=groups.at[slot],
                    send_sem=obs_send.at[9 + b + 1],
                    recv_sem=obs_recv.at[2],
                    device_id={"gx": target},
                    device_id_type=MESH,
                )
            )

        if act_local:

            @pl.when(jnp.logical_and(at_fold, target == col))
            def _():
                pltpu.make_async_copy(packed, groups.at[slot], obs_recv.at[2]).start()

    for a in (0, 1, -1):
        for b in (-1, 0, 1):
            obs_plain(a, b, lambda copy: copy.start())
    for b in (-1, 0, 1):
        obs_fold(b, lambda copy: copy.start(), True)
    pltpu.make_async_copy(packed, groups.at[4], obs_recv.at[1]).start()

    side = 4

    def distance(d):
        dy, dz = d // side, d % side
        return min(dy, side - dy) + min(dz, side - dz)

    order = sorted(range(1, ncols), key=distance)
    yy = col // side
    zz = lax.rem(col, side)

    def states_of(target, c):
        return states.at[
            :, :, pl.ds(pl.multiple_of(c * RB, RB), RB), pl.ds(pl.multiple_of(target * TX, TX), TX)
        ]

    def issue(c, _):
        pltpu.make_async_copy(
            states_of(col, c), fields.at[c, pl.ds(col * share, share)], state_recv.at[c]
        ).start()
        for d in order:
            target = lax.rem(yy + d // side, side) * side + lax.rem(zz + d % side, side)
            pltpu.make_async_remote_copy(
                src_ref=states_of(target, c),
                dst_ref=fields.at[c, pl.ds(col * share, share)],
                send_sem=state_send.at[c],
                recv_sem=state_recv.at[c],
                device_id={"gx": target},
                device_id_type=MESH,
            ).start()
        return 0

    lax.fori_loop(0, chunks, issue, 0)

    @pl.when(row == 0)
    def _():
        groups[0:3] = jnp.zeros((3, PK, LANES), BF16)

    @pl.when(row > 0)
    def _():
        three = groups.at[0:3]
        pltpu.make_async_copy(three, three, obs_recv.at[0]).wait()

    for a in (0, 1):
        three = groups.at[3 * (a + 1) : 3 * (a + 2)]
        pltpu.make_async_copy(three, three, obs_recv.at[a + 1]).wait()

    live = lax.broadcasted_iota(jnp.int32, (LANES, LANES), 0) < members
    for g in range(9):
        part = jnp.concatenate([groups[g], jnp.zeros((LANES - PK, LANES), BF16)], axis=0)
        right[:, g * LANES : (g + 1) * LANES] = jnp.where(
            live, part.astype(F32), 0.0
        ).astype(BF16)

    eye = (
        lax.broadcasted_iota(jnp.int32, (members, LANES), 0)
        == lax.broadcasted_iota(jnp.int32, (members, LANES), 1)
    ).astype(F32)
    width_x = float(TX * ncols)
    height_y = float(TY * nrows)

    def weigh(c):
        block_y = (
            row * TY + c * RB + lax.broadcasted_iota(jnp.int32, (RB, LANES), 0)
        ).astype(F32)
        for g in range(9):
            a, b = g // 3 - 1, g % 3 - 1
            around = groups[g].astype(F32)
            src_row = row + a
            src_col = wrap(col + b, ncols)
            local_row = around[members + 1 : members + 2]
            local_col = around[members + 2 : members + 3]
            if a == 1:
                folded = row == nrows - 1
                src_row = jnp.where(folded, nrows - 1, src_row)
                src_col = jnp.where(folded, wrap(ncols - 1 - col + b, ncols), src_col)
            obs_y = (src_row * TY).astype(F32) + local_row
            obs_x = (src_col * TX).astype(F32) + local_col
            if a == 1:
                turn = jnp.where(folded, 1.0, 0.0)
                obs_y = obs_y + turn * (2.0 * height_y - 1.0 - 2.0 * obs_y)
                obs_x = obs_x + turn * (width_x - 1.0 - 2.0 * obs_x)
            gap_y = obs_y - block_y
            offset = obs_x - (col * TX).astype(F32)
            offset = jnp.where(offset < 0.0, offset + width_x, offset)
            gap_x = jnp.where(
                offset < TX, 0.0, jnp.minimum(offset - (TX - 1.0), width_x - offset)
            )
            radius = float(TY // 2)
            scaled = jnp.minimum(1.0, (gap_x * gap_x + gap_y * gap_y) / (radius * radius))
            taper = (1.0 - scaled) * (1.0 - scaled)
            for r in range(RB):
                weighted[r * PK : (r + 1) * PK, g * LANES : (g + 1) * LANES] = (
                    around * taper[r : r + 1]
                ).astype(BF16)
        products[...] = lax.dot_general(
            weighted[...],
            right[...],
            (((1,), (1,)), ((), ())),
            preferred_element_type=F32,
        )

    def transforms(rows):
        scale, iterate, inverse = {}, {}, {}
        for r in rows:
            cov = products[r * PK : r * PK + members]
            system = eye + tall(cov).T[:members] * (1.0 / (members - 1.0))
            total = jnp.sum(jnp.sum(system * system, axis=0, keepdims=True), axis=1, keepdims=True)
            scale[r] = jnp.sqrt(total)
            iterate[r] = system / scale[r]
        for r in rows:
            inverse[r] = 1.5 * eye - 0.5 * iterate[r]
        iterate = {r: product(split(iterate[r]), split(inverse[r])) for r in rows}
        for sweep in range(1, NS_ITERS):
            inv = {r: split(inverse[r]) for r in rows}
            itr = {r: split(iterate[r]) for r in rows}
            both = {r: product(inv[r], itr[r]) for r in rows}
            cor = {r: split(1.5 * eye - 0.5 * both[r]) for r in rows}
            if sweep < NS_ITERS - 1:
                iterate = {r: product(itr[r], cor[r]) for r in rows}
            inverse = {r: product(cor[r], inv[r]) for r in rows}
        for r in rows:
            inv = split(inverse[r])
            projected = products[r * PK + members : r * PK + members + 8]
            once = product(split(projected), inv)
            mean = product(split(once), inv)[0:1]
            tmat[r] = (
                inverse[r] / jnp.sqrt(scale[r]) + mean / (scale[r] * (members - 1.0))
            ).astype(BF16)

    def analyse(c):
        for pair in range(levels // 2):
            averages = []
            for half in range(2):
                lev = 2 * pair + half
                field = fields[c, :, lev].astype(F32)
                average = jnp.sum(field, axis=0) * (1.0 / members)
                averages.append(average)
                spread[half] = (field - average[None]).reshape(members * RB, LANES)
            for r in range(RB):
                perturb = jnp.concatenate(
                    [
                        tall(spread[half, pl.ds(r, members, stride=RB), :].astype(BF16))
                        for half in range(2)
                    ],
                    axis=1,
                )
                mix = jnp.dot(tmat[r], perturb, preferred_element_type=F32)
                for half in range(2):
                    mixed[half, pl.ds(r, members, stride=RB), :] = mix[
                        :, half * LANES : (half + 1) * LANES
                    ]
            for half in range(2):
                lev = 2 * pair + half
                value = mixed[half].reshape(members, RB, LANES) + averages[half][None]
                out[c, :, lev] = value.astype(BF16)

    def step(c, _):
        weigh(c)
        for first in range(0, RB, 4):
            transforms(range(first, first + 4))
        pltpu.make_async_copy(fields.at[c], fields.at[c], state_recv.at[c]).wait()
        analyse(c)
        return 0

    lax.fori_loop(0, chunks, step, 0)

    def sent(c, _):
        part = fields.at[c, 0 : (ncols - 1) * share]
        pltpu.make_async_copy(part, part, state_send.at[c]).wait()
        return 0

    lax.fori_loop(0, chunks, sent, 0)
    for a in (0, 1, -1):
        for b in (-1, 0, 1):
            obs_plain(a, b, lambda copy: copy.wait_send())
    for b in (-1, 0, 1):
        obs_fold(b, lambda copy: copy.wait_send(), False)


def place(chunks, rows, done, out, sem):
    copies = [
        pltpu.make_async_copy(done.at[c], out.at[:, :, c * rows : (c + 1) * rows, :], sem.at[c])
        for c in range(chunks)
    ]
    for copy in copies:
        copy.start()
    for copy in copies:
        copy.wait()


def body(states, obs_pert, obs_innov, obs_cell, obs_count):
    members = obs_pert.shape[0]
    slots = obs_pert.shape[2]
    levels = states.shape[1]
    ncols = lax.axis_size("gx")
    nrows = lax.axis_size("gy")
    filled = lax.broadcasted_iota(jnp.int32, (1, slots), 1) < obs_count
    perturbs = jnp.where(filled, obs_pert[:, 0, :], jnp.zeros((), BF16))
    innovation = jnp.where(filled, obs_innov, jnp.zeros((), BF16))
    packed = jnp.concatenate(
        [
            perturbs,
            innovation,
            (obs_cell // TX).astype(BF16),
            (obs_cell % TX).astype(BF16),
            jnp.zeros((PK - members - 3, slots), BF16),
        ],
        axis=0,
    )
    chunks = TY // RB
    done = pl.pallas_call(
        functools.partial(kernel, members, levels, nrows, ncols),
        out_shape=jax.ShapeDtypeStruct((chunks, members, levels, RB, TX), BF16),
        in_specs=[pl.BlockSpec(memory_space=pl.ANY), pl.BlockSpec(memory_space=pl.ANY)],
        out_specs=pl.BlockSpec(memory_space=pltpu.VMEM),
        scratch_shapes=[
            pltpu.VMEM((chunks, members, levels, RB, TX), BF16),
            pltpu.VMEM((9, PK, LANES), BF16),
            pltpu.VMEM((LANES, 9 * LANES), BF16),
            pltpu.VMEM((RB * PK, 9 * LANES), BF16),
            pltpu.VMEM((RB * PK, LANES), F32),
            pltpu.VMEM((RB, members, LANES), BF16),
            pltpu.VMEM((2, members * RB, LANES), F32),
            pltpu.VMEM((2, members * RB, LANES), F32),
            pltpu.SemaphoreType.DMA,
            pltpu.SemaphoreType.DMA((chunks,)),
            pltpu.SemaphoreType.DMA((chunks,)),
            pltpu.SemaphoreType.DMA((12,)),
            pltpu.SemaphoreType.DMA((3,)),
        ],
        compiler_params=pltpu.CompilerParams(
            collective_id=0, has_side_effects=True, vmem_limit_bytes=40 << 20
        ),
        name="exchange",
    )(states, packed)
    return pl.pallas_call(
        functools.partial(place, chunks, RB),
        out_shape=jax.ShapeDtypeStruct((members, levels, TY, TX), BF16),
        in_specs=[pl.BlockSpec(memory_space=pltpu.VMEM)],
        out_specs=pl.BlockSpec(memory_space=pl.ANY),
        scratch_shapes=[pltpu.SemaphoreType.DMA((chunks,))],
        compiler_params=pltpu.CompilerParams(vmem_limit_bytes=16 << 20),
        name="place",
    )(done)


def solution(mesh):
    return jax.shard_map(
        body,
        mesh=mesh,
        in_specs=(
            P("gx", None, "gy", None),
            P(None, "gy", "gx"),
            P("gy", "gx"),
            P("gy", "gx"),
            P("gy", "gx"),
        ),
        out_specs=P(None, None, "gy", "gx"),
        check_vma=False,
    )
```

profile of v0, /device:TPU:75, one launch (start us, length us, event | category | flops | bytes accessed | tf_op | source)
XLA Modules:
  0.0 147.2 jit_solution(936072298302981543)
XLA Ops:
  0.7 0.7 compare_select_fusion
  1.3 0.7 fusion
  2.0 0.7 bitcast_select_fusion
  2.7 0.2 concatenate.3.packed
  2.9 140.3 %exchange.1.done = bf16[8,80,8,8,128]{4,3,2,1,0:T(8,128)(2,1)S(1)} custom-call(bf16[5,8,64,2048]{3,2,1,0:T(8,128)(2,1)} %states.1, bf16[96,128]{1,0:T(8,128)(2,1)S(1)} %concatenate.3.packed), custom_call_target="tpu_custom_call" | custom-call | tf_op jit(solution)/shard_map/exchange/pallas_call | solution.py:360
  143.2 4.0 %place.1 = bf16[80,8,64,128]{3,2,1,0:T(8,128)(2,1)} custom-call(bf16[8,80,8,8,128]{4,3,2,1,0:T(8,128)(2,1)S(1)} %exchange.1.done), custom_call_target="tpu_custom_call" | custom-call | tf_op jit(solution)/shard_map/place/pallas_call | solution.py:385
  (2 shorter events, 0.0 us)
where the time goes:
time: 147 us
  Pallas kernels  144 us (98%)
  other arithmetic  2.07 us (1%)
    pallas_call x1, Pallas kernels, body(): pl.pallas_call(functools.partial(kernel, members, levels, nrows, ncols),...  140 us
    pallas_call x1, Pallas kernels, body(): pl.pallas_call(functools.partial(place, chunks, RB), out_shape=jax.ShapeD...  4.04 us

commit v1 on v0

--- a/solution.py
+++ b/solution.py
@@ -49,23 +49,54 @@
     return both[:, :LANES] + both[:, LANES:]
 
 
+def analyse(members, fields, tmat, spread, mixed, results, pair):
+    averages = []
+    for half in range(2):
+        field = fields[:, 2 * pair + half].astype(F32)
+        average = jnp.sum(field, axis=0) * (1.0 / members)
+        averages.append(average)
+        spread[half] = (field - average[None]).reshape(members * RB, LANES)
+    for r in range(RB):
+        perturb = jnp.concatenate(
+            [
+                tall(spread[half, pl.ds(r, members, stride=RB), :].astype(BF16))
+                for half in range(2)
+            ],
+            axis=1,
+        )
+        mix = jnp.dot(tmat[r], perturb, preferred_element_type=F32)
+        for half in range(2):
+            mixed[half, pl.ds(r, members, stride=RB), :] = mix[
+                :, half * LANES : (half + 1) * LANES
+            ]
+    for half in range(2):
+        value = mixed[half].reshape(members, RB, LANES) + averages[half][None]
+        results[:, 2 * pair + half] = value.astype(BF16)
+
+
 def kernel(
     members,
     levels,
     nrows,
     ncols,
     states,
+    obs_pert,
+    obs_innov,
+    obs_cell,
+    count,
+    fields,
+    tmat,
+    pert,
+    innov,
+    cell,
     packed,
-    out,
-    fields,
     groups,
     right,
     weighted,
     products,
-    tmat,
     spread,
     mixed,
-    own_sem,
+    obs_in,
     state_send,
     state_recv,
     obs_send,
@@ -75,6 +106,15 @@
     row = lax.axis_index("gy")
     share = members // ncols
     chunks = TY // RB
+
+    loads = [
+        pltpu.make_async_copy(source, into, obs_in.at[i])
+        for i, (source, into) in enumerate(
+            ((obs_pert, pert), (obs_innov, innov), (obs_cell, cell))
+        )
+    ]
+    for load in loads:
+        load.start()
 
     barrier = pltpu.get_barrier_semaphore()
 
@@ -140,6 +180,59 @@
             def _():
                 pltpu.make_async_copy(packed, groups.at[slot], obs_recv.at[2]).start()
 
+    side = 4
+
+    def distance(d):
+        dy, dz = d // side, d % side
+        return min(dy, side - dy) + min(dz, side - dz)
+
+    order = sorted(range(1, ncols), key=distance)
+    yy = col // side
+    zz = lax.rem(col, side)
+    odd = lax.rem(row, 2) == 1
+
+    def states_of(target, c, some):
+        return states.at[
+            :, some, pl.ds(pl.multiple_of(c * RB, RB), RB), pl.ds(pl.multiple_of(target * TX, TX), TX)
+        ]
+
+    def issue(c, _):
+        pltpu.make_async_copy(
+            states_of(col, c, slice(None)), fields.at[c, pl.ds(col * share, share)], state_recv.at[c]
+        ).start()
+        for half in range(2):
+            some = pl.ds(half * (levels // 2), levels // 2)
+            for d in order:
+                dy, dz = d // side, d % side
+                dy = jnp.where(odd, side - dy, dy)
+                dz = jnp.where(odd, side - dz, dz)
+                target = lax.rem(yy + dy, side) * side + lax.rem(zz + dz, side)
+                pltpu.make_async_remote_copy(
+                    src_ref=states_of(target, c, some),
+                    dst_ref=fields.at[c, pl.ds(col * share, share), some],
+                    send_sem=state_send.at[c],
+                    recv_sem=state_recv.at[c],
+                    device_id={"gx": target},
+                    device_id_type=MESH,
+                ).start()
+        return 0
+
+    issue(0, 0)
+    for load in loads:
+        load.wait()
+    filled = lax.broadcasted_iota(jnp.int32, (1, LANES), 1) < count[0, 0]
+    packed[0:members] = jnp.where(filled, pert[...].astype(F32), 0.0).astype(BF16)
+    cells = cell[...]
+    packed[members:] = jnp.concatenate(
+        [
+            jnp.where(filled, innov[...].astype(F32), 0.0),
+            lax.shift_right_logical(cells, 7).astype(F32),
+            lax.bitwise_and(cells, 127).astype(F32),
+            jnp.zeros((PK - members - 3, LANES), F32),
+        ],
+        axis=0,
+    ).astype(BF16)
+    issue(1, 0)
     for a in (0, 1, -1):
         for b in (-1, 0, 1):
             obs_plain(a, b, lambda copy: copy.start())
@@ -147,38 +240,7 @@
         obs_fold(b, lambda copy: copy.start(), True)
     pltpu.make_async_copy(packed, groups.at[4], obs_recv.at[1]).start()
 
-    side = 4
-
-    def distance(d):
-        dy, dz = d // side, d % side
-        return min(dy, side - dy) + min(dz, side - dz)
-
-    order = sorted(range(1, ncols), key=distance)
-    yy = col // side
-    zz = lax.rem(col, side)
-
-    def states_of(target, c):
-        return states.at[
-            :, :, pl.ds(pl.multiple_of(c * RB, RB), RB), pl.ds(pl.multiple_of(target * TX, TX), TX)
-        ]
-
-    def issue(c, _):
-        pltpu.make_async_copy(
-            states_of(col, c), fields.at[c, pl.ds(col * share, share)], state_recv.at[c]
-        ).start()
-        for d in order:
-            target = lax.rem(yy + d // side, side) * side + lax.rem(zz + d % side, side)
-            pltpu.make_async_remote_copy(
-                src_ref=states_of(target, c),
-                dst_ref=fields.at[c, pl.ds(col * share, share)],
-                send_sem=state_send.at[c],
-                recv_sem=state_recv.at[c],
-                device_id={"gx": target},
-                device_id_type=MESH,
-            ).start()
-        return 0
-
-    lax.fori_loop(0, chunks, issue, 0)
+    lax.fori_loop(2, chunks, issue, 0)
 
     @pl.when(row == 0)
     def _():
@@ -276,39 +338,18 @@
                 inverse[r] / jnp.sqrt(scale[r]) + mean / (scale[r] * (members - 1.0))
             ).astype(BF16)
 
-    def analyse(c):
-        for pair in range(levels // 2):
-            averages = []
-            for half in range(2):
-                lev = 2 * pair + half
-                field = fields[c, :, lev].astype(F32)
-                average = jnp.sum(field, axis=0) * (1.0 / members)
-                averages.append(average)
-                spread[half] = (field - average[None]).reshape(members * RB, LANES)
-            for r in range(RB):
-                perturb = jnp.concatenate(
-                    [
-                        tall(spread[half, pl.ds(r, members, stride=RB), :].astype(BF16))
-                        for half in range(2)
-                    ],
-                    axis=1,
-                )
-                mix = jnp.dot(tmat[r], perturb, preferred_element_type=F32)
-                for half in range(2):
-                    mixed[half, pl.ds(r, members, stride=RB), :] = mix[
-                        :, half * LANES : (half + 1) * LANES
-                    ]
-            for half in range(2):
-                lev = 2 * pair + half
-                value = mixed[half].reshape(members, RB, LANES) + averages[half][None]
-                out[c, :, lev] = value.astype(BF16)
-
     def step(c, _):
         weigh(c)
         for first in range(0, RB, 4):
             transforms(range(first, first + 4))
         pltpu.make_async_copy(fields.at[c], fields.at[c], state_recv.at[c]).wait()
-        analyse(c)
+
+        @pl.when(c < chunks - 1)
+        def _():
+            here = fields.at[c]
+            for pair in range(levels // 2):
+                analyse(members, here, tmat, spread, mixed, here, pair)
+
         return 0
 
     lax.fori_loop(0, chunks, step, 0)
@@ -326,13 +367,23 @@
         obs_fold(b, lambda copy: copy.wait_send(), False)
 
 
-def place(chunks, rows, done, out, sem):
+def place(members, levels, chunks, fields, tmat, out, spread, mixed, last, sem):
     copies = [
-        pltpu.make_async_copy(done.at[c], out.at[:, :, c * rows : (c + 1) * rows, :], sem.at[c])
-        for c in range(chunks)
+        pltpu.make_async_copy(fields.at[c], out.at[:, :, c * RB : (c + 1) * RB, :], sem.at[c])
+        for c in range(chunks - 1)
     ]
     for copy in copies:
         copy.start()
+    c = chunks - 1
+    for pair in range(levels // 2):
+        analyse(members, fields.at[c], tmat, spread, mixed, last, pair)
+        some = slice(2 * pair, 2 * pair + 2)
+        copies.append(
+            pltpu.make_async_copy(
+                last.at[:, some], out.at[:, some, c * RB : (c + 1) * RB, :], sem.at[c + pair]
+            )
+        )
+        copies[-1].start()
     for copy in copies:
         copy.wait()
 
@@ -343,35 +394,32 @@
     levels = states.shape[1]
     ncols = lax.axis_size("gx")
     nrows = lax.axis_size("gy")
-    filled = lax.broadcasted_iota(jnp.int32, (1, slots), 1) < obs_count
-    perturbs = jnp.where(filled, obs_pert[:, 0, :], jnp.zeros((), BF16))
-    innovation = jnp.where(filled, obs_innov, jnp.zeros((), BF16))
-    packed = jnp.concatenate(
-        [
-            perturbs,
-            innovation,
-            (obs_cell // TX).astype(BF16),
-            (obs_cell % TX).astype(BF16),
-            jnp.zeros((PK - members - 3, slots), BF16),
-        ],
-        axis=0,
-    )
     chunks = TY // RB
-    done = pl.pallas_call(
+    hbm = pl.BlockSpec(memory_space=pltpu.HBM)
+    vmem = pl.BlockSpec(memory_space=pltpu.VMEM)
+    work = [
+        pltpu.VMEM((2, members * RB, LANES), F32),
+        pltpu.VMEM((2, members * RB, LANES), F32),
+    ]
+    fields, tmat = pl.pallas_call(
         functools.partial(kernel, members, levels, nrows, ncols),
-        out_shape=jax.ShapeDtypeStruct((chunks, members, levels, RB, TX), BF16),
-        in_specs=[pl.BlockSpec(memory_space=pl.ANY), pl.BlockSpec(memory_space=pl.ANY)],
-        out_specs=pl.BlockSpec(memory_space=pltpu.VMEM),
+        out_shape=(
+            jax.ShapeDtypeStruct((chunks, members, levels, RB, TX), BF16),
+            jax.ShapeDtypeStruct((RB, members, LANES), BF16),
+        ),
+        in_specs=[hbm] * 4 + [pl.BlockSpec(memory_space=pltpu.SMEM)],
+        out_specs=(vmem, vmem),
         scratch_shapes=[
-            pltpu.VMEM((chunks, members, levels, RB, TX), BF16),
+            pltpu.VMEM((members, slots), BF16),
+            pltpu.VMEM((1, slots), BF16),
+            pltpu.VMEM((1, slots), jnp.int32),
+            pltpu.VMEM((PK, LANES), BF16),
             pltpu.VMEM((9, PK, LANES), BF16),
             pltpu.VMEM((LANES, 9 * LANES), BF16),
             pltpu.VMEM((RB * PK, 9 * LANES), BF16),
             pltpu.VMEM((RB * PK, LANES), F32),
-            pltpu.VMEM((RB, members, LANES), BF16),
-            pltpu.VMEM((2, members * RB, LANES), F32),
-            pltpu.VMEM((2, members * RB, LANES), F32),
-            pltpu.SemaphoreType.DMA,
+            *work,
+            pltpu.SemaphoreType.DMA((3,)),
             pltpu.SemaphoreType.DMA((chunks,)),
             pltpu.SemaphoreType.DMA((chunks,)),
             pltpu.SemaphoreType.DMA((12,)),
@@ -381,16 +429,27 @@
             collective_id=0, has_side_effects=True, vmem_limit_bytes=40 << 20
         ),
         name="exchange",
-    )(states, packed)
+    )(
+        states,
+        *(
+            pltpu.with_memory_space_constraint(value, pltpu.HBM)
+            for value in (obs_pert.reshape(members, slots), obs_innov, obs_cell)
+        ),
+        obs_count,
+    )
     return pl.pallas_call(
-        functools.partial(place, chunks, RB),
+        functools.partial(place, members, levels, chunks),
         out_shape=jax.ShapeDtypeStruct((members, levels, TY, TX), BF16),
-        in_specs=[pl.BlockSpec(memory_space=pltpu.VMEM)],
-        out_specs=pl.BlockSpec(memory_space=pl.ANY),
-        scratch_shapes=[pltpu.SemaphoreType.DMA((chunks,))],
-        compiler_params=pltpu.CompilerParams(vmem_limit_bytes=16 << 20),
+        in_specs=[vmem, vmem],
+        out_specs=hbm,
+        scratch_shapes=[
+            *work,
+            pltpu.VMEM((members, levels, RB, TX), BF16),
+            pltpu.SemaphoreType.DMA((chunks - 1 + levels // 2,)),
+        ],
+        compiler_params=pltpu.CompilerParams(vmem_limit_bytes=24 << 20),
         name="place",
-    )(done)
+    )(fields, tmat)
 
 
 def solution(mesh):

time: 147 us -> 129 us (0.88); the launches traced: 147 us -> 127 us
  Pallas kernels: 144 us -> 127 us
  other arithmetic: 2.07 us -> 0 us
    pallas_call x1, Pallas kernels: 140 us -> 123 us  [body(): pl.pallas_call(functools.partial(kernel, members, levels, nrows, ncols),...]
where the time goes in v1:
time: 129 us; the launch traced here: 127 us
  Pallas kernels  127 us (98%)
    pallas_call x1, Pallas kernels, body(): pl.pallas_call(functools.partial(kernel, members, levels, nrows, ncols),...  123 us
    pallas_call x1, Pallas kernels, body(): pl.pallas_call(functools.partial(place, members, levels, chunks), out_sha...  4.04 us

profile of v1, /device:TPU:75, one launch (start us, length us, event | category | flops | bytes accessed | tf_op | source)
XLA Modules:
  0.0 127.2 jit_solution(926857887736393087)
XLA Ops:
  0.7 122.5 %exchange.1 = (bf16[8,80,8,8,128]{4,3,2,1,0:T(8,128)(2,1)S(1)}, bf16[8,80,128]{2,1,0:T(8,128)(2,1)S(1)}) custom-call(bf16[5,8,64,2048]{3,2,1,0:T(8,128)(2,1)} %states.1, bf16[80,128]{1,0:T(8,128)(2,1)} %bitcast.1, bf16[1,128]{1,0:T(2,128)(2,1)} %obs_innov.1, s32[1,128]{1,0:T(1,128)} %obs_cell.1, s32[1,1]{1,0:T(1,128)S(6)} %copy.6.count), custom_call_target="tpu_custom_call" | custom-call | tf_op jit(solution)/shard_map/exchange/pallas_call | solution.py:404
  123.2 4.0 %place.1 = bf16[80,8,64,128]{3,2,1,0:T(8,128)(2,1)} custom-call(bf16[8,80,8,8,128]{4,3,2,1,0:T(8,128)(2,1)S(1)} %get-tuple-element.7.fields, bf16[8,80,128]{2,1,0:T(8,128)(2,1)S(1)} %get-tuple-element.8.tmat), custom_call_target="tpu_custom_call" | custom-call | tf_op jit(solution)/shard_map/place/pallas_call | solution.py:440

commit v2 on v1

--- a/solution.py
+++ b/solution.py
@@ -113,8 +113,6 @@
             ((obs_pert, pert), (obs_innov, innov), (obs_cell, cell))
         )
     ]
-    for load in loads:
-        load.start()
 
     barrier = pltpu.get_barrier_semaphore()
 
@@ -130,6 +128,8 @@
             for b in (-1, 0, 1):
                 greet({"gx": wrap(col + b, ncols), "gy": row + a})
 
+    for load in loads:
+        load.start()
     inner = jnp.logical_and(row > 0, row < nrows - 1)
     pl.semaphore_wait(barrier, ncols - 1 + jnp.where(inner, 6, 3))
 

time: 129 us -> 129 us (level)
  no operation moved by 1% of the time
where the time goes in v2:
time: 129 us; the launch traced here: 127 us
  Pallas kernels  127 us (98%)
    pallas_call x1, Pallas kernels, body(): pl.pallas_call(functools.partial(kernel, members, levels, nrows, ncols),...  123 us
    pallas_call x1, Pallas kernels, body(): pl.pallas_call(functools.partial(place, members, levels, chunks), out_sha...  4.04 us

profile of v2, /device:TPU:75, one launch (start us, length us, event | category | flops | bytes accessed | tf_op | source)
XLA Modules:
  0.0 127.2 jit_solution(17014915528246543246)
XLA Ops:
  0.7 122.5 %exchange.1 = (bf16[8,80,8,8,128]{4,3,2,1,0:T(8,128)(2,1)S(1)}, bf16[8,80,128]{2,1,0:T(8,128)(2,1)S(1)}) custom-call(bf16[5,8,64,2048]{3,2,1,0:T(8,128)(2,1)} %states.1, bf16[80,128]{1,0:T(8,128)(2,1)} %bitcast.1, bf16[1,128]{1,0:T(2,128)(2,1)} %obs_innov.1, s32[1,128]{1,0:T(1,128)} %obs_cell.1, s32[1,1]{1,0:T(1,128)S(6)} %copy.6.count), custom_call_target="tpu_custom_call" | custom-call | tf_op jit(solution)/shard_map/exchange/pallas_call | solution.py:404
  123.2 4.0 %place.1 = bf16[80,8,64,128]{3,2,1,0:T(8,128)(2,1)} custom-call(bf16[8,80,8,8,128]{4,3,2,1,0:T(8,128)(2,1)S(1)} %get-tuple-element.7.fields, bf16[8,80,128]{2,1,0:T(8,128)(2,1)S(1)} %get-tuple-element.8.tmat), custom_call_target="tpu_custom_call" | custom-call | tf_op jit(solution)/shard_map/place/pallas_call | solution.py:440
